TPU v7x, 256 devices: a whole 4x4x8 slice. The times are simulated.
256 devices in a mesh: var: 32 (over y, x, core), tp: 8 (over z).
Axes of the slice: x: 4, y: 4, z: 8, core: 2. Of those that a mesh axis runs over, the one named last changes fastest.
Arguments:
- tokens: bfloat16 [32768, 8192], P('var', 'tp'), may hold values from -6 to 6
- kv_weight: bfloat16 [8192, 2048], P('tp'), may hold values from -0.0625 to 0.0625
- factor_a: bfloat16 [64, 8192, 128], P('var', 'tp'), may hold values from -0.0625 to 0.0625
- factor_scale: bfloat16 [64, 128], P('var'), may hold values from 0.29882812 to 3
- factor_b: bfloat16 [64, 128, 2048], P('var', None, 'tp'), may hold values from -0.5 to 0.5
- counts: int32 [32, 64], replicated, may hold values from 0 to 64, as said below
Outputs:
- kv_out: bfloat16 [32768, 2048], P('var', 'tp')
Inputs may be any that keep to these rules, and one draw needn't show every extreme that they name: `counts`: each row sums to 1024. Owner o holds variants 2 * o to 2 * o + 1; in every row those variants together have at most 64 tokens, and in every draw one owner has exactly 64 tokens in every row.
All inputs are finite; a program needn't handle non-finite values.
Results may differ from a plain program's by a relative error of at most 0.011.
Values may be sent and summed in bfloat16 or wider, within the bound.
No kernel may reach another device: no remote copies, remote signals or barrier semaphores. Data moves between devices by JAX's collectives and lax.ppermute only.
A program may use at most 128 MiB of HBM per device.

v0:
```python
import jax
import jax.numpy as jnp
from jax import lax
from jax.sharding import PartitionSpec as P


def in_blocks(value, dim, length):
    before, after = (value.shape[:dim], value.shape[dim + 1 :])
    return jnp.moveaxis(value.reshape(*before, length, -1, *after), dim, 0)


def sum_at_owner(value, axis, dim):
    length = lax.axis_size(axis)
    parts = lax.all_to_all(in_blocks(value, dim, length), axis, 0, 0, tiled=True)
    return jnp.sum(parts.astype(jnp.float32), axis=0)


def copy_for_each(value, axis):
    copies = jnp.broadcast_to(value, (lax.axis_size(axis), *value.shape))
    return lax.all_to_all(copies, axis, split_axis=0, concat_axis=0, tiled=True)


def joined_along(parts, dim):
    parts = jnp.moveaxis(parts, 0, dim)
    lengths = parts.shape
    return parts.reshape(*lengths[:dim], lengths[dim] * lengths[dim + 1], *lengths[dim + 2 :])


def gathered_copies(value, axis, dim):
    parts = copy_for_each(value, axis)
    return joined_along(parts, dim)


def pick_table(block_counts, capacity):
    slot_ids = jnp.arange(capacity, dtype=jnp.int32)
    var_dev = block_counts.shape[1]
    bounds = jnp.cumsum(block_counts, axis=1)
    local_pick = jnp.sum(
        (slot_ids[None, :, None] >= bounds[:, None, : var_dev - 1]).astype(jnp.int32), axis=2
    )
    return (local_pick[:, :, None] == jnp.arange(var_dev, dtype=jnp.int32)[None, None, :]).astype(
        jnp.float32
    )


def rank_project(blocks, picker, factor_in, equation):
    products = jnp.einsum(equation, blocks, factor_in, preferred_element_type=jnp.float32)
    return jnp.sum(products * picker[..., None], axis=2)


def expand_rank(rank_part, picker, scale_table, factor_out, equation):
    rank_share = sum_at_owner(rank_part.astype(jnp.bfloat16), "tp", 1)
    share_rows = rank_share.shape[1]
    offset = lax.axis_index("tp") * share_rows
    pick_share = lax.dynamic_slice_in_dim(picker, offset, share_rows, 1)
    scaled_share = (rank_share * jnp.sum(pick_share[..., None] * scale_table, axis=2)).astype(
        jnp.bfloat16
    )
    scaled = gathered_copies(scaled_share, "tp", 1)
    outputs = jnp.einsum(equation, scaled, factor_out, preferred_element_type=jnp.float32)
    return jnp.sum(outputs * picker[..., None], axis=2).astype(jnp.bfloat16)


def body(tokens, kv_weight, factor_a, factor_scale, factor_b, counts):
    var_count = lax.axis_size("var")
    owner_index = lax.axis_index("var")
    tok_rows = tokens.shape[0]
    var_dev = factor_a.shape[0]
    capacity = 2 * tok_rows // var_count
    partial_value = jnp.dot(tokens, kv_weight, preferred_element_type=jnp.float32)
    base_part = lax.psum_scatter(
        partial_value.astype(jnp.bfloat16), "tp", scatter_dimension=1, tiled=True
    ).astype(jnp.float32)
    own_counts = lax.dynamic_index_in_dim(counts, owner_index, 0, keepdims=False)
    owner_counts = own_counts.reshape(var_count, var_dev)
    starts = jnp.cumsum(own_counts) - own_counts
    first_rows = starts.reshape(var_count, var_dev)[:, 0]
    slot_ids = jnp.arange(capacity, dtype=jnp.int32)
    inside = slot_ids[None, :] < jnp.sum(owner_counts, axis=1)[:, None]
    row_index = jnp.clip(first_rows[:, None] + slot_ids[None, :], 0, tok_rows - 1)
    outgoing = jnp.where(inside[:, :, None], tokens[row_index], jnp.zeros((), tokens.dtype))
    every_in, every_out, every_scale = (
        lax.all_gather(factor_a, "var", axis=0, tiled=True),
        lax.all_gather(factor_b, "var", axis=0, tiled=True),
        lax.all_gather(factor_scale, "var", axis=0, tiled=True),
    )
    picker = pick_table(owner_counts, capacity)
    factor_in = every_in.reshape(var_count, var_dev, every_in.shape[1], every_in.shape[2])
    factor_out = every_out.reshape(var_count, var_dev, every_out.shape[1], every_out.shape[2])
    scale_table = every_scale.astype(jnp.float32).reshape(
        var_count, 1, var_dev, every_scale.shape[1]
    )
    rank_part = rank_project(outgoing, picker, factor_in, "ocd,ovdr->ocvr")
    delta_blocks = expand_rank(rank_part, picker, scale_table, factor_out, "ocr,ovrk->ocvk")
    ends_at = jnp.cumsum(own_counts)
    position = jnp.arange(tok_rows, dtype=jnp.int32)
    variant = jnp.sum((ends_at[None, :] <= position[:, None]).astype(jnp.int32), axis=1)
    owner_of = variant // var_dev
    owner_hot = owner_of[:, None] == jnp.arange(var_count, dtype=jnp.int32)[None, :]
    owner_first = jnp.sum(jnp.where(owner_hot, first_rows[None, :], 0), axis=1)
    flat_index = owner_of * capacity + position - owner_first
    delta_rows = delta_blocks.reshape(var_count * capacity, delta_blocks.shape[2])[flat_index]
    return (base_part + delta_rows.astype(jnp.float32)).astype(jnp.bfloat16)


def solution(mesh):
    return jax.shard_map(
        body,
        mesh=mesh,
        in_specs=(
            P("var", "tp"),
            P("tp", None),
            P("var", "tp", None),
            P("var", None),
            P("var", None, "tp"),
            P(),
        ),
        out_specs=P("var", "tp"),
        check_vma=False,
    )
```

profile of v0, /device:TPU:1, one launch (start us, length us, event | category | flops | bytes accessed | tf_op | source)
XLA Modules:
  0.0 176.4 jit_solution(6263837088870079892)
XLA Ops:
  7.4 0.7 all-gather.4.cloned.1.call-update
  8.1 0.7 all-gather.6.cloned.1.call-update
  9.0 8.2 %convolution_convert_fusion = bf16[1024,2048]{1,0:T(8,128)(2,1)} fusion(bf16[1024,1024]{1,0:T(8,128)(2,1)S(1)} %copy-done, bf16[1024,2048]{1,0:T(8,128)(2,1)} %param.7), kind=kOutput, calls=%fused_computation.7 | convolution fusion | flops 4297064448 | bytes 10485760 | tf_op jit(solution)/shard_map/dot_general | solution.py:70
  17.2 0.7 fusion.13
  17.9 0.1 reshape.219
  18.0 0.2 reduce_window_sum.19
  18.2 0.1 reduce_sum.71
  18.3 0.1 copy.18
  18.4 0.1 reduce-window.4
  18.5 0.1 reduce.1
  18.6 0.1 reshape.221
  18.7 0.1 fusion.9
  18.9 0.1 reshape.228
  19.0 9.7 %gather_fusion = bf16[2048,1024]{1,0:T(8,128)(2,1)} fusion(bf16[1024,1024]{1,0:T(8,128)(2,1)S(1)} %copy-done, s32[2048]{0:T(1024)S(1)} %broadcast_clamp_fusion), kind=kCustom, calls=%fused_computation | custom fusion | bytes 8396800 | tf_op jit(solution)/shard_map/gather | solution.py:81
  28.7 0.1 slice_reduce_fusion
  29.0 63.6 %all-gather.4.cloned.1.call-done = bf16[64,1024,128]{2,1,0:T(8,128)(2,1)} async-done(((bf16[2,1024,128]{2,1,0:T(8,128)(2,1)}), bf16[64,1024,128]{2,1,0:T(8,128)(2,1)}) %all-gather.4.cloned.1.call-update) | async-done | bytes 16777232 | tf_op jit(solution)/shard_map/all_gather | solution.py:83
  92.6 10.2 %multiply_reduce_fusion.1 = bf16[32,64,128]{2,1,0:T(8,128)(2,1)S(1)} fusion(f32[32,64,2]{1,2,0:T(2,128)S(1)} %compare_convert_fusion, bf16[32,2,1024,128]{3,2,1,0:T(8,128)(2,1)} %bitcast.47, bf16[32,64,1024]{2,1,0:T(8,128)(2,1)} %bitcast.40, pred[32,64]{1,0:T(8,128)(4,1)S(1)} %iota_compare_fusion.3), kind=kOutput, calls=%fused_computation.8 | convolution fusion | flops 1076625408 | bytes 21514240 | tf_op jit(solution)/shard_map/ocd,ovdr->ocvr/dot_general | solution.py:47
  102.8 0.9 copy.19
  103.7 6.7 %all-to-all-start = ((bf16[8,32,8,128]{3,2,1,0:T(8,128)(2,1)}), bf16[8,32,8,128]{3,2,1,0:T(8,128)(2,1)S(1)}, u32[]{:S(2)}, u32[]{:S(2)}) async-start(bf16[8,32,8,128]{3,2,1,0:T(8,128)(2,1)} %copy.19), calls=%async_computation.1 | async-start | bytes 1048576 | tf_op jit(solution)/shard_map/all_to_all | solution.py:14
  110.4 21.2 %all-gather = bf16[32,2,128]{2,1,0:T(2,128)(2,1)S(1)} all-gather(bf16[1,2,128]{2,1,0:T(2,128)(2,1)S(1)} %bitcast.46), channel_id=1, replica_groups=mesh['var'=32,'tp'=8] {'var'}, dimensions={0}, use_global_device_ids=true | all-gather | bytes 16896 | tf_op jit(solution)/shard_map/all_gather | solution.py:85
  131.7 0.1 constant_dynamic-slice_fusion
  131.8 0.1 multiply_reduce_fusion.2
  132.0 0.9 broadcast_in_dim.24
  132.9 6.9 %all-to-all-start.1 = ((bf16[8,32,8,128]{3,2,1,0:T(8,128)(2,1)}), bf16[8,32,8,128]{3,2,1,0:T(8,128)(2,1)S(1)}, u32[]{:S(2)}, u32[]{:S(2)}) async-start(bf16[8,32,8,128]{3,2,1,0:T(8,128)(2,1)} %broadcast_in_dim.24), calls=%async_computation.2 | async-start | bytes 1048576 | tf_op jit(solution)/shard_map/all_to_all | solution.py:20
  139.8 0.1 convert_reduce_fusion.1
  139.9 0.1 select_reduce_fusion
  140.1 5.7 %all-gather.6.cloned.1.call-done = bf16[64,128,256]{2,1,0:T(8,128)(2,1)} async-done(((bf16[2,128,256]{2,1,0:T(8,128)(2,1)}), bf16[64,128,256]{2,1,0:T(8,128)(2,1)}) %all-gather.6.cloned.1.call-update) | async-done | bytes 4194320 | tf_op jit(solution)/shard_map/all_gather | solution.py:84
  145.7 12.0 %all-to-all-done.1 = bf16[8,32,8,128]{3,2,1,0:T(8,128)(2,1)S(1)} async-done(((bf16[8,32,8,128]{3,2,1,0:T(8,128)(2,1)}), bf16[8,32,8,128]{3,2,1,0:T(8,128)(2,1)S(1)}, u32[]{:S(2)}, u32[]{:S(2)}) %all-to-all-start.1) | async-done | bytes 524320 | tf_op jit(solution)/shard_map/all_to_all | solution.py:20
  157.8 0.8 copy-done.1
  158.6 3.3 %multiply_reduce_fusion = bf16[32,64,256]{2,1,0:T(8,128)(2,1)S(1)} fusion(bf16[32,2,128,256]{3,2,1,0:T(8,128)(2,1)} %bitcast.41, f32[32,64,2]{1,2,0:T(2,128)S(1)} %compare_convert_fusion, bf16[8,32,8,128]{3,2,1,0:T(8,128)(2,1)} %copy-done.1), kind=kOutput, calls=%fused_computation.4 | convolution fusion | flops 270008320 | bytes 5783552 | tf_op jit(solution)/shard_map/ocr,ovrk->ocvk/dot_general | solution.py:60
  161.9 5.0 %gather_fusion.1 = bf16[1024,256]{1,0:T(8,128)(2,1)} fusion(bf16[2048,256]{1,0:T(8,128)(2,1)S(1)} %bitcast.39, s32[1024]{0:T(1024)S(1)} %broadcast_clamp_fusion.1), kind=kCustom, calls=%fused_computation.1 | custom fusion | bytes 1052672 | tf_op jit(solution)/shard_map/gather | solution.py:102
  166.8 2.1 %add_convert_fusion = bf16[1024,256]{1,0:T(8,128)(2,1)} fusion(bf16[1024,256]{1,0:T(8,128)(2,1)} %gather_fusion.1, bf16[1024,256]{1,0:T(8,128)(2,1)} %reduce-scatter.2.cloned.1.call-done), kind=kLoop, calls=%fused_computation.10 | loop fusion | flops 1048576 | bytes 1572864 | tf_op jit(solution)/shard_map/convert_element_type | solution.py:103
  (22 shorter events, 0.6 us)
Async XLA Ops:
  7.4 1.6 copy-start
  7.4 85.2 %all-gather.4.cloned.1.call-start = ((), (), s32[]{:S(2)}) async-start(), calls=%async_computation.4 | async-start | bytes 17301504 | tf_op jit(solution)/shard_map/all_gather | solution.py:83
  8.1 137.6 %all-gather.6.cloned.1.call-start = ((), (), s32[]{:S(2)}) async-start(), calls=%async_computation.5 | async-start | bytes 4325376 | tf_op jit(solution)/shard_map/all_gather | solution.py:84
  8.8 158.0 %reduce-scatter.2.cloned.1.call-start = ((), (), s32[]{:S(2)}) async-start(), calls=%async_computation.3 | async-start | bytes 4718592 | tf_op jit(solution)/shard_map/reduce_scatter | solution.py:71
  92.6 17.9 %copy-start.2 = (bf16[2,128]{1,0:T(2,128)(2,1)S(1)}, bf16[2,128]{1,0:T(2,128)(2,1)}, u32[]{:S(2)}) copy-start(bf16[2,128]{1,0:T(2,128)(2,1)} %param.9) | copy-start | bytes 1540
  103.7 28.2 %all-to-all-start = ((bf16[8,32,8,128]{3,2,1,0:T(8,128)(2,1)}), bf16[8,32,8,128]{3,2,1,0:T(8,128)(2,1)S(1)}, u32[]{:S(2)}, u32[]{:S(2)}) async-start(bf16[8,32,8,128]{3,2,1,0:T(8,128)(2,1)} %copy.19), calls=%async_computation.1 | async-start | bytes 1048576 | tf_op jit(solution)/shard_map/all_to_all | solution.py:14
  132.9 24.9 %all-to-all-start.1 = ((bf16[8,32,8,128]{3,2,1,0:T(8,128)(2,1)}), bf16[8,32,8,128]{3,2,1,0:T(8,128)(2,1)S(1)}, u32[]{:S(2)}, u32[]{:S(2)}) async-start(bf16[8,32,8,128]{3,2,1,0:T(8,128)(2,1)} %broadcast_in_dim.24), calls=%async_computation.2 | async-start | bytes 1048576 | tf_op jit(solution)/shard_map/all_to_all | solution.py:20
  157.8 0.8 copy-start.1
Sparse Core Ops, SparseCore 0:
  10.7 81.7 all-gather.3
  95.1 50.5 all-gather.5
Sparse Core Ops, SparseCore 1:
  17.3 59.0 reduce-scatter.1
where the time goes:
time: 177 us; the launch traced here: 176 us
  waiting for transfers between devices  82.7 us (47%)
  matrix products  21.7 us (12%)
  blocking collectives  21.2 us (12%)
  local copies, waits for them, and re-layouts  18.6 us (11%)
  between operations  15 us (8%)
  starting transfers between devices  13.7 us (8%)
  other arithmetic  3.44 us (2%)
    all_gather x1, waiting for transfers between devices, body(): lax.all_gather(factor_a, 'var', axis=0, tiled=True)  63.6 us
    all_gather x1, blocking collectives, body(): lax.all_gather(factor_scale, 'var', axis=0, tiled=True)  21.2 us
    all_to_all x1, waiting for transfers between devices, copy_for_each(): return lax.all_to_all(copies, axis, split_axis=0, concat_axis=0, tiled=True)  12 us
    dot_general x1, matrix products, rank_project(): jnp.einsum(equation, blocks, factor_in, preferred_element_type=jnp.float32)  10.2 us
    gather x1, local copies, waits for them, and re-layouts, body(): tokens[row_index]  9.7 us
    dot_general x1, matrix products, body(): jnp.dot(tokens, kv_weight, preferred_element_type=jnp.float32)  8.22 us
    all_to_all x1, starting transfers between devices, copy_for_each(): return lax.all_to_all(copies, axis, split_axis=0, concat_axis=0, tiled=True)  6.89 us
    all_to_all x1, starting transfers between devices, sum_at_owner(): lax.all_to_all(in_blocks(value, dim, length), axis, 0, 0, tiled=True)  6.73 us
  transfers between devices with their start and end apart: 5, of which 3 were waited for; matrix products, arithmetic and copies ran while one was open for 23% of the time, Pallas kernels for 0%

commit v1 on v0

--- a/solution.py
+++ b/solution.py
@@ -2,6 +2,11 @@
 import jax.numpy as jnp
 from jax import lax
 from jax.sharding import PartitionSpec as P
+
+
+def tiled_gather(x, axis, dim):
+    copies = jnp.concatenate([x] * lax.axis_size(axis), axis=dim)
+    return lax.all_to_all(copies, axis, dim, dim, tiled=True)
 
 
 def in_blocks(value, dim, length):
@@ -82,7 +87,7 @@
     every_in, every_out, every_scale = (
         lax.all_gather(factor_a, "var", axis=0, tiled=True),
         lax.all_gather(factor_b, "var", axis=0, tiled=True),
-        lax.all_gather(factor_scale, "var", axis=0, tiled=True),
+        tiled_gather(factor_scale, "var", 0),
     )
     picker = pick_table(owner_counts, capacity)
     factor_in = every_in.reshape(var_count, var_dev, every_in.shape[1], every_in.shape[2])

time: 177 us -> 170 us (0.960)
  blocking collectives: 21.2 us -> 0 us
  local copies, waits for them, and re-layouts: 18.6 us -> 24 us
  starting transfers between devices: 13.7 us -> 18.9 us
  waiting for transfers between devices: 82.7 us -> 86.4 us
    all_gather x1 -> x0, blocking collectives: 21.2 us -> none  [body(): lax.all_gather(factor_scale, 'var', axis=0, tiled=True)]
    all_to_all x1, waiting for transfers between devices: 0.01 us -> 17.7 us  [sum_at_owner(): lax.all_to_all(in_blocks(value, dim, length), axis, 0, 0, tiled=True)]
    all_gather x1, waiting for transfers between devices: 63.6 us -> 49.7 us  [body(): lax.all_gather(factor_a, 'var', axis=0, tiled=True)]
    all_to_all x0 -> x1, starting transfers between devices: none -> 8.58 us  [tiled_gather(): return lax.all_to_all(copies, axis, dim, dim, tiled=True)]
    all_to_all x1, waiting for transfers between devices: 12 us -> 4.98 us  [copy_for_each(): return lax.all_to_all(copies, axis, split_axis=0, concat_axis=0, tiled=True)]
    all_gather x1, waiting for transfers between devices: 5.66 us -> 12.6 us  [body(): lax.all_gather(factor_b, 'var', axis=0, tiled=True)]
    concatenate x0 -> x1, local copies, waits for them, and re-layouts: none -> 4.77 us  [tiled_gather(): copies = jnp.concatenate([x] * lax.axis_size(axis), axis=dim)]
    all_to_all x1, starting transfers between devices: 6.89 us -> 3.49 us  [copy_for_each(): return lax.all_to_all(copies, axis, split_axis=0, concat_axis=0, tiled=True)]
  transfers between devices with their start and end apart: 5 -> 6, of which waited for: 3 -> 4; matrix products, arithmetic and copies ran while one was open for 23% -> 27% of each run, Pallas kernels for 0% -> 0%
where the time goes in v1:
time: 170 us; the launch traced here: 169 us
  waiting for transfers between devices  86.4 us (51%)
  local copies, waits for them, and re-layouts  24 us (14%)
  matrix products  21.7 us (13%)
  starting transfers between devices  18.9 us (11%)
  between operations  15 us (9%)
  other arithmetic  3.44 us (2%)
    all_gather x1, waiting for transfers between devices, body(): lax.all_gather(factor_a, 'var', axis=0, tiled=True)  49.7 us
    all_to_all x1, waiting for transfers between devices, sum_at_owner(): lax.all_to_all(in_blocks(value, dim, length), axis, 0, 0, tiled=True)  17.7 us
    all_gather x1, waiting for transfers between devices, body(): lax.all_gather(factor_b, 'var', axis=0, tiled=True)  12.6 us
    dot_general x1, matrix products, rank_project(): jnp.einsum(equation, blocks, factor_in, preferred_element_type=jnp.float32)  10.2 us
    gather x1, local copies, waits for them, and re-layouts, body(): tokens[row_index]  9.7 us
    all_to_all x1, starting transfers between devices, tiled_gather(): return lax.all_to_all(copies, axis, dim, dim, tiled=True)  8.58 us
    dot_general x1, matrix products, body(): jnp.dot(tokens, kv_weight, preferred_element_type=jnp.float32)  8.22 us
    all_to_all x1, starting transfers between devices, sum_at_owner(): lax.all_to_all(in_blocks(value, dim, length), axis, 0, 0, tiled=True)  6.73 us
  transfers between devices with their start and end apart: 6, of which 4 were waited for; matrix products, arithmetic and copies ran while one was open for 27% of the time, Pallas kernels for 0%

profile of v1, /device:TPU:1, one launch (start us, length us, event | category | flops | bytes accessed | tf_op | source)
XLA Modules:
  0.0 169.4 jit_solution(7242241947404643095)
XLA Ops:
  7.4 0.7 all-gather.3.cloned.1.call-update
  8.1 0.7 all-gather.5.cloned.1.call-update
  9.0 8.2 %convolution_convert_fusion = bf16[1024,2048]{1,0:T(8,128)(2,1)} fusion(bf16[1024,1024]{1,0:T(8,128)(2,1)S(1)} %copy-done, bf16[1024,2048]{1,0:T(8,128)(2,1)} %param.7), kind=kOutput, calls=%fused_computation.7 | convolution fusion | flops 4297064448 | bytes 10485760 | tf_op jit(solution)/shard_map/dot_general | solution.py:75
  17.2 0.6 copy-done.2
  17.8 4.8 %concatenate.3 = bf16[64,128]{1,0:T(8,128)(2,1)} concatenate(bf16[2,128]{1,0:T(2,128)(2,1)S(1)} %copy-done.2, bf16[2,128]{1,0:T(2,128)(2,1)S(1)} %copy-done.2, bf16[2,128]{1,0:T(2,128)(2,1)S(1)} %copy-done.2, bf16[2,128]{1,0:T(2,128)(2,1)S(1)} %copy-done.2, bf16[2,128]{1,0:T(2,128)(2,1)S(1)} %copy-done.2, bf16[2,128]{1,0:T(2,128)(2,1)S(1)} %copy-done.2, ...), dimensions={0} | concatenate | bytes 32768 | tf_op jit(solution)/shard_map/concatenate | solution.py:8
  22.6 8.6 %all-to-all-start.1 = ((bf16[32,2,128]{2,1,0:T(2,128)(2,1)}), bf16[32,2,128]{2,1,0:T(2,128)(2,1)S(1)}, u32[]{:S(2)}, u32[]{:S(2)}) async-start(bf16[32,2,128]{2,1,0:T(2,128)(2,1)} %bitcast.7), calls=%async_computation.2 | async-start | bytes 32768 | tf_op jit(solution)/shard_map/all_to_all | solution.py:9
  31.2 0.7 fusion.13
  31.9 0.1 reshape.223
  32.0 0.2 reduce_window_sum.19
  32.2 0.1 reduce_sum.71
  32.3 0.1 copy.18
  32.4 0.1 reduce-window.4
  32.5 0.1 reduce.1
  32.6 0.1 reshape.225
  32.7 0.1 fusion.9
  33.0 9.7 %gather_fusion = bf16[2048,1024]{1,0:T(8,128)(2,1)} fusion(bf16[1024,1024]{1,0:T(8,128)(2,1)S(1)} %copy-done, s32[2048]{0:T(1024)S(1)} %broadcast_clamp_fusion), kind=kCustom, calls=%fused_computation | custom fusion | bytes 8396800 | tf_op jit(solution)/shard_map/gather | solution.py:86
  42.7 0.1 slice_reduce_fusion
  43.0 49.7 %all-gather.3.cloned.1.call-done = bf16[64,1024,128]{2,1,0:T(8,128)(2,1)} async-done(((bf16[2,1024,128]{2,1,0:T(8,128)(2,1)}), bf16[64,1024,128]{2,1,0:T(8,128)(2,1)}) %all-gather.3.cloned.1.call-update) | async-done | bytes 16777232 | tf_op jit(solution)/shard_map/all_gather | solution.py:88
  92.6 10.2 %multiply_reduce_fusion.1 = bf16[32,64,128]{2,1,0:T(8,128)(2,1)S(1)} fusion(f32[32,64,2]{1,2,0:T(2,128)S(1)} %compare_convert_fusion, bf16[32,2,1024,128]{3,2,1,0:T(8,128)(2,1)} %bitcast.46, bf16[32,64,1024]{2,1,0:T(8,128)(2,1)} %bitcast.40, pred[32,64]{1,0:T(8,128)(4,1)S(1)} %iota_compare_fusion.3), kind=kOutput, calls=%fused_computation.8 | convolution fusion | flops 1076625408 | bytes 21514240 | tf_op jit(solution)/shard_map/ocd,ovdr->ocvr/dot_general | solution.py:52
  102.9 0.9 copy.19
  103.7 6.7 %all-to-all-start = ((bf16[8,32,8,128]{3,2,1,0:T(8,128)(2,1)}), bf16[8,32,8,128]{3,2,1,0:T(8,128)(2,1)S(1)}, u32[]{:S(2)}, u32[]{:S(2)}) async-start(bf16[8,32,8,128]{3,2,1,0:T(8,128)(2,1)} %copy.19), calls=%async_computation.1 | async-start | bytes 1048576 | tf_op jit(solution)/shard_map/all_to_all | solution.py:19
  110.6 0.1 multiply_reduce_fusion.2
  110.7 17.7 %all-to-all-done = bf16[8,32,8,128]{3,2,1,0:T(8,128)(2,1)S(1)} async-done(((bf16[8,32,8,128]{3,2,1,0:T(8,128)(2,1)}), bf16[8,32,8,128]{3,2,1,0:T(8,128)(2,1)S(1)}, u32[]{:S(2)}, u32[]{:S(2)}) %all-to-all-start) | async-done | bytes 524320 | tf_op jit(solution)/shard_map/all_to_all | solution.py:19
  128.5 0.9 broadcast_in_dim.24
  129.4 3.5 %all-to-all-start.2 = ((bf16[8,32,8,128]{3,2,1,0:T(8,128)(2,1)}), bf16[8,32,8,128]{3,2,1,0:T(8,128)(2,1)S(1)}, u32[]{:S(2)}, u32[]{:S(2)}) async-start(bf16[8,32,8,128]{3,2,1,0:T(8,128)(2,1)} %broadcast_in_dim.24), calls=%async_computation.3 | async-start | bytes 1048576 | tf_op jit(solution)/shard_map/all_to_all | solution.py:25
  132.9 0.1 convert_reduce_fusion.1
  133.2 12.6 %all-gather.5.cloned.1.call-done = bf16[64,128,256]{2,1,0:T(8,128)(2,1)} async-done(((bf16[2,128,256]{2,1,0:T(8,128)(2,1)}), bf16[64,128,256]{2,1,0:T(8,128)(2,1)}) %all-gather.5.cloned.1.call-update) | async-done | bytes 4194320 | tf_op jit(solution)/shard_map/all_gather | solution.py:89
  145.8 5.0 %all-to-all-done.2 = bf16[8,32,8,128]{3,2,1,0:T(8,128)(2,1)S(1)} async-done(((bf16[8,32,8,128]{3,2,1,0:T(8,128)(2,1)}), bf16[8,32,8,128]{3,2,1,0:T(8,128)(2,1)S(1)}, u32[]{:S(2)}, u32[]{:S(2)}) %all-to-all-start.2) | async-done | bytes 524320 | tf_op jit(solution)/shard_map/all_to_all | solution.py:25
  150.8 0.8 copy-done.1
  151.6 3.3 %multiply_reduce_fusion = bf16[32,64,256]{2,1,0:T(8,128)(2,1)S(1)} fusion(bf16[32,2,128,256]{3,2,1,0:T(8,128)(2,1)} %bitcast.41, f32[32,64,2]{1,2,0:T(2,128)S(1)} %compare_convert_fusion, bf16[8,32,8,128]{3,2,1,0:T(8,128)(2,1)} %copy-done.1), kind=kOutput, calls=%fused_computation.4 | convolution fusion | flops 270008320 | bytes 5783552 | tf_op jit(solution)/shard_map/ocr,ovrk->ocvk/dot_general | solution.py:65
  154.9 5.0 %gather_fusion.1 = bf16[1024,256]{1,0:T(8,128)(2,1)} fusion(bf16[2048,256]{1,0:T(8,128)(2,1)S(1)} %bitcast.39, s32[1024]{0:T(1024)S(1)} %broadcast_clamp_fusion.1), kind=kCustom, calls=%fused_computation.1 | custom fusion | bytes 1052672 | tf_op jit(solution)/shard_map/gather | solution.py:107
  159.8 2.1 %add_convert_fusion = bf16[1024,256]{1,0:T(8,128)(2,1)} fusion(bf16[1024,256]{1,0:T(8,128)(2,1)} %gather_fusion.1, bf16[1024,256]{1,0:T(8,128)(2,1)} %reduce-scatter.2.cloned.1.call-done), kind=kLoop, calls=%fused_computation.10 | loop fusion | flops 1048576 | bytes 1572864 | tf_op jit(solution)/shard_map/convert_element_type | solution.py:108
  (24 shorter events, 0.8 us)
Async XLA Ops:
  7.4 1.6 copy-start
  7.4 85.3 %all-gather.3.cloned.1.call-start = ((), (), s32[]{:S(2)}) async-start(), calls=%async_computation.5 | async-start | bytes 17301504 | tf_op jit(solution)/shard_map/all_gather | solution.py:88
  8.1 137.7 %all-gather.5.cloned.1.call-start = ((), (), s32[]{:S(2)}) async-start(), calls=%async_computation.6 | async-start | bytes 4325376 | tf_op jit(solution)/shard_map/all_gather | solution.py:89
  8.8 151.0 %reduce-scatter.2.cloned.1.call-start = ((), (), s32[]{:S(2)}) async-start(), calls=%async_computation.4 | async-start | bytes 4718592 | tf_op jit(solution)/shard_map/reduce_scatter | solution.py:76
  17.2 0.7 copy-start.2
  22.6 81.1 %all-to-all-start.1 = ((bf16[32,2,128]{2,1,0:T(2,128)(2,1)}), bf16[32,2,128]{2,1,0:T(2,128)(2,1)S(1)}, u32[]{:S(2)}, u32[]{:S(2)}) async-start(bf16[32,2,128]{2,1,0:T(2,128)(2,1)} %bitcast.7), calls=%async_computation.2 | async-start | bytes 32768 | tf_op jit(solution)/shard_map/all_to_all | solution.py:9
  103.7 24.7 %all-to-all-start = ((bf16[8,32,8,128]{3,2,1,0:T(8,128)(2,1)}), bf16[8,32,8,128]{3,2,1,0:T(8,128)(2,1)S(1)}, u32[]{:S(2)}, u32[]{:S(2)}) async-start(bf16[8,32,8,128]{3,2,1,0:T(8,128)(2,1)} %copy.19), calls=%async_computation.1 | async-start | bytes 1048576 | tf_op jit(solution)/shard_map/all_to_all | solution.py:19
  129.4 21.4 %all-to-all-start.2 = ((bf16[8,32,8,128]{3,2,1,0:T(8,128)(2,1)}), bf16[8,32,8,128]{3,2,1,0:T(8,128)(2,1)S(1)}, u32[]{:S(2)}, u32[]{:S(2)}) async-start(bf16[8,32,8,128]{3,2,1,0:T(8,128)(2,1)} %broadcast_in_dim.24), calls=%async_computation.3 | async-start | bytes 1048576 | tf_op jit(solution)/shard_map/all_to_all | solution.py:25
  150.8 0.8 copy-start.1
Sparse Core Ops, SparseCore 0:
  10.7 81.8 all-gather.2
  95.2 50.5 all-gather.4
Sparse Core Ops, SparseCore 1:
  17.3 58.9 reduce-scatter.1
